TPU v7x, 128 devices: a whole 4x4x4 slice. The times are simulated.
128 devices in a mesh: gz: 2 (over core), gx: 16 (over z, y), gy: 4 (over x).
Axes of the slice: x: 4, y: 4, z: 4, core: 2. Of those that a mesh axis runs over, the one named last changes fastest.
Arguments:
- pair_repr: bfloat16 [8, 384, 384, 128], P('gz', 'gx', 'gy'), may hold values from -9 to 9
- seq_lengths: int32 [8], replicated, may hold values from 96 to 384
- weight_in: bfloat16 [128, 640], replicated, may hold values from -0.5 to 0.5
- weight_out: bfloat16 [128, 128], replicated, may hold values from -0.5 to 0.5
Outputs:
- updated: bfloat16 [8, 384, 384, 128], P('gz', 'gx', 'gy')
- magnitude: float32 [], replicated
All inputs are finite; a program needn't handle non-finite values.
Results may differ from a plain program's by a relative error of at most 0.0034.
Values may be sent and summed in bfloat16 or wider, within the bound.
A program may use at most 320 MiB of HBM per device.

v0:
```python
import jax
import jax.numpy as jnp
from jax import lax
from jax.sharding import Mesh
from jax.sharding import PartitionSpec as P

GX = ("gx_0", "gx_1")
GZ_GX_GY = ("gz", "gx_0", "gx_1", "gy")


def in_order(parts, dim):
    lengths = list(parts.shape[1:])
    lengths[dim] *= parts.shape[0]
    return jnp.moveaxis(parts, 0, dim).reshape(lengths)


def from_everyone(array, axis):
    size = lax.axis_size(axis)
    return lax.all_to_all(
        jnp.broadcast_to(array[None], (size, *array.shape)), axis, 0, 0, tiled=True
    )


def gathered_copies(array, axis, dim):
    return in_order(from_everyone(array, axis), dim)


def by_axis(array, axes):
    for axis in axes:
        array = lax.psum(array, axis)
    return array


def layer_norm(values):
    mean_value = jnp.mean(values, axis=-1, keepdims=True)
    centered = values - mean_value
    variance = jnp.mean(centered * centered, axis=-1, keepdims=True)
    return centered * lax.rsqrt(variance + 1e-05)


def per_device(pair_repr, seq_lengths, weight_in, weight_out):
    batch_dev, row_count, col_count, channels = pair_repr.shape
    hidden = weight_out.shape[0]
    row_first = lax.axis_index(GX) * row_count
    col_first = lax.axis_index("gy") * col_count
    my_lengths = lax.dynamic_slice_in_dim(seq_lengths, lax.axis_index("gz") * batch_dev, batch_dev)
    row_live = (
        (row_first + jnp.arange(row_count, dtype=jnp.int32))[None, :] < my_lengths[:, None]
    ).astype(jnp.float32)
    col_live = (
        (col_first + jnp.arange(col_count, dtype=jnp.int32))[None, :] < my_lengths[:, None]
    ).astype(jnp.float32)
    pair_mask = row_live[:, :, None, None] * col_live[:, None, :, None]
    normed = layer_norm(pair_repr.astype(jnp.float32)).astype(jnp.bfloat16)
    proj = jnp.dot(normed.reshape(-1, channels), weight_in, preferred_element_type=jnp.float32)
    proj = proj.reshape(batch_dev, row_count, col_count, 4 * hidden + channels)
    left_proj = (
        pair_mask * jax.nn.sigmoid(proj[..., hidden : 2 * hidden]) * proj[..., :hidden]
    ).astype(jnp.bfloat16)
    right_proj = (
        pair_mask
        * jax.nn.sigmoid(proj[..., 3 * hidden : 4 * hidden])
        * proj[..., 2 * hidden : 3 * hidden]
    ).astype(jnp.bfloat16)
    gate_values = jax.nn.sigmoid(proj[..., 4 * hidden :])
    left_rows = gathered_copies(left_proj, "gy", 2)
    left_turned = lax.all_to_all(left_rows, GX, split_axis=2, concat_axis=1, tiled=True)
    triangle = jnp.einsum(
        "bkic,bkjc->bijc",
        left_turned,
        lax.all_gather(right_proj, GX, axis=1, tiled=True),
        preferred_element_type=jnp.float32,
    )
    tri_normed = layer_norm(triangle).astype(jnp.bfloat16)
    projected = jnp.dot(
        tri_normed.reshape(-1, hidden), weight_out, preferred_element_type=jnp.float32
    )
    update = pair_mask * gate_values * projected.reshape(batch_dev, row_count, col_count, channels)
    updated = (pair_repr.astype(jnp.float32) + update).astype(jnp.bfloat16)
    mag_total = by_axis(jnp.sum(jnp.abs(updated.astype(jnp.float32))), GZ_GX_GY)
    entry_count = (
        batch_dev
        * lax.axis_size("gz")
        * row_count
        * lax.axis_size(GX)
        * col_count
        * lax.axis_size("gy")
        * channels
    )
    magnitude = mag_total / float(entry_count)
    return (updated, magnitude)


def solution(mesh):
    finer = Mesh(
        mesh.devices.reshape(mesh.shape["gz"], 4, 4, mesh.shape["gy"]), ("gz", "gx_0", "gx_1", "gy")
    )
    in_specs = (P("gz", GX, "gy", None), P(), P(), P())
    out_specs = (P("gz", GX, "gy", None), P())
    return jax.shard_map(
        per_device, mesh=finer, in_specs=in_specs, out_specs=out_specs, check_vma=False
    )
```

profile of v0, /device:TPU:1, one launch (start us, length us, event | category | flops | bytes accessed | tf_op | source)
XLA Modules:
  0.0 513.3 jit_solution(9637882763817909198)
XLA Ops:
  7.2 0.0 copy-start
  7.2 0.0 all-gather.2.cloned.1.call-start
  7.3 0.7 dynamic_slice.3
  8.0 0.1 compare_convert_fusion.1
  8.1 0.1 compare_convert_fusion
  8.1 2.6 convert_reduce_fusion
  10.7 4.4 fusion.2
  15.1 0.1 broadcast_multiply_fusion.2
  15.2 0.0 copy-done
  15.2 7.4 %fusion.22 = f32[4,24,96,640]{3,2,1,0:T(8,128)S(1)} fusion(bf16[4,24,96,128]{3,2,1,0:T(8,128)(2,1)} %param.4, f32[4,24,96]{2,1,0:T(8,128)S(1)} %add_rsqrt_fusion.1, f32[4,24,96]{2,1,0:T(8,128)S(1)} %broadcast_multiply_fusion.1, bf16[128,640]{1,0:T(8,128)(2,1)S(1)} %copy-done), kind=kOutput, calls=%fused_computation.35 | convolution fusion | flops 1514668032 | bytes 26189824 | tf_op jit(solution)/shard_map/dot_general | solution.py:55
  22.6 5.8 %fusion.5 = (bf16[4,24,96,128]{3,2,1,0:T(8,128)(2,1)}, bf16[4,24,96,128]{3,2,1,0:T(8,128)(2,1)}) fusion(f32[4,24,96,640]{3,2,1,0:T(8,128)S(1)} %fusion.22, f32[4,24,96]{2,1,0:T(8,128)S(1)} %broadcast_multiply_fusion.2), kind=kLoop, calls=%fused_computation.13 | loop fusion | flops 14155776 | bytes 23629824 | tf_op jit(solution)/shard_map/convert_element_type | solution.py:59
  28.5 3.4 copy-done.3
  31.9 0.0 all-gather.2.cloned.1.call-update
  31.9 3.5 broadcast_in_dim.2
  35.4 108.9 %all_to_all.23 = bf16[4,4,24,96,128]{4,3,2,1,0:T(8,128)(2,1)} all-to-all(bf16[4,4,24,96,128]{4,3,2,1,0:T(8,128)(2,1)S(1)} %broadcast_in_dim.2), channel_id=1, replica_groups=mesh['gz'=2,'gx_0'=4,'gx_1'=4,'gy'=4] {'gy'}, dimensions={0} | all-to-all | bytes 18874368 | tf_op jit(solution)/shard_map/all_to_all | solution.py:19
  144.3 10.4 %copy.12 = bf16[4,4,24,96,128]{4,3,0,2,1:T(8,128)(2,1)} copy(bf16[4,4,24,96,128]{4,3,2,1,0:T(8,128)(2,1)} %all_to_all.23) | data formatting | bytes 18874368 | tf_op jit(solution)/shard_map/all_to_all | solution.py:19
  154.7 13.8 %copy.13 = bf16[4,24,384,128]{3,1,0,2:T(8,128)(2,1)} copy(bf16[4,24,384,128]{3,2,1,0:T(8,128)(2,1)} %bitcast.28) | data formatting | bytes 18874368 | tf_op jit(solution)/shard_map/reshape | solution.py:14
  168.5 188.0 %all_to_all.24 = bf16[4,24,384,128]{3,1,0,2:T(8,128)(2,1)} all-to-all(bf16[4,24,384,128]{3,1,0,2:T(8,128)(2,1)} %copy.13), channel_id=1, replica_groups=mesh['gz'=2,'gx_0'=4,'gx_1'=4,'gy'=4] {'gx_0','gx_1'}, dimensions={2} | all-to-all | bytes 18874368 | tf_op jit(solution)/shard_map/all_to_all | solution.py:67
  356.4 13.4 %copy.15 = bf16[4,16,24,24,128]{4,3,2,1,0:T(8,128)(2,1)} copy(bf16[4,16,24,24,128]{4,2,0,3,1:T(8,128)(2,1)} %bitcast.29) | data formatting | bytes 18874368 | tf_op jit(solution)/shard_map/all_to_all | solution.py:67
  369.9 14.0 %copy.17 = bf16[4,384,24,128]{1,2,3,0:T(8,128)(2,1)} copy(bf16[4,384,24,128]{3,2,1,0:T(8,128)(2,1)} %bitcast.30) | data formatting | bytes 18874368 | tf_op jit(solution)/shard_map/all_to_all | solution.py:67
  383.9 57.9 %copy.16 = bf16[4,384,96,128]{2,1,3,0:T(8,128)(2,1)} copy(bf16[4,384,96,128]{3,2,1,0:T(8,128)(2,1)} %all-gather.2.cloned.1.call-done) | data formatting | bytes 75497472 | tf_op jit(solution)/shard_map/all_gather | solution.py:71
  441.7 22.7 %bitcast_reduce_fusion = (f32[4,24,96]{2,1,0:T(8,128)S(1)}, f32[4,128,96,24]{2,3,1,0:T(8,128)}) fusion(bf16[4,384,96,128]{2,1,3,0:T(8,128)(2,1)} %copy.16, bf16[4,384,24,128]{1,2,3,0:T(8,128)(2,1)} %copy.17), kind=kOutput, calls=%fused_computation.4 | convolution fusion | flops 907140096 | bytes 51941376 | tf_op jit(solution)/shard_map/bkic,bkjc->bijc/dot_general | solution.py:68
  464.4 3.8 multiply_reduce_fusion
  468.2 0.8 copy-done.2
  469.0 0.7 multiply_convert_fusion
  469.7 1.0 copy-done.4
  470.7 0.0 copy-done.5
  470.7 6.4 %abs_reduce_fusion = (f32[]{:T(128)}, bf16[4,24,96,128]{3,2,1,0:T(8,128)(2,1)}) fusion(bf16[128,128]{1,0:T(8,128)(2,1)S(1)} %copy-done.5, bf16[4,24,96,128]{2,1,3,0:T(8,128)(2,1)S(1)} %multiply_convert_fusion, f32[4,24,96,640]{3,2,1,0:T(8,128)} %copy-done.3, f32[4,24,96]{2,1,0:T(8,128)S(1)} %broadcast_multiply_fusion.2, ...), kind=kOutput, calls=%fused_computation.32 | convolution fusion | flops 314966016 | bytes 11866116 | tf_op jit(solution)/shard_map/dot_general | solution.py:75
  477.1 4.2 psum.28
  481.3 7.1 %psum.29 = f32[]{:T(128)} all-reduce(f32[]{:T(128)} %psum.28), channel_id=1, replica_groups=mesh['gz'=2,'gx_0'=4,'gx_1'=4,'gy'=4] {'gx_0'}, use_global_device_ids=true, to_apply=%region_6.0 | all-reduce | flops 1 | bytes 8 | tf_op jit(solution)/shard_map/psum | solution.py:30
  488.4 7.3 %psum.30 = f32[]{:T(128)} all-reduce(f32[]{:T(128)} %psum.29), channel_id=1, replica_groups=mesh['gz'=2,'gx_0'=4,'gx_1'=4,'gy'=4] {'gx_1'}, use_global_device_ids=true, to_apply=%region_7.0 | all-reduce | flops 1 | bytes 8 | tf_op jit(solution)/shard_map/psum | solution.py:30
  495.7 9.0 %psum.31 = f32[]{:T(128)} all-reduce(f32[]{:T(128)} %psum.30), channel_id=1, replica_groups=mesh['gz'=2,'gx_0'=4,'gx_1'=4,'gy'=4] {'gy'}, use_global_device_ids=true, to_apply=%region_8.0 | all-reduce | flops 1 | bytes 8 | tf_op jit(solution)/shard_map/psum | solution.py:30
  (13 shorter events, 0.1 us)
Async XLA Ops:
  7.2 8.1 %copy-start = (bf16[128,640]{1,0:T(8,128)(2,1)S(1)}, bf16[128,640]{1,0:T(8,128)(2,1)}, u32[]{:S(2)}) copy-start(bf16[128,640]{1,0:T(8,128)(2,1)} %param.6) | copy-start | bytes 491524
  7.2 376.7 %all-gather.2.cloned.1.call-start = ((), (), s32[]{:S(2)}) async-start(), calls=%async_computation.2 | async-start | bytes 40108032 | tf_op jit(solution)/shard_map/all_gather | solution.py:71
  22.6 9.3 %copy-start.3 = (f32[4,24,96,640]{3,2,1,0:T(8,128)}, f32[4,24,96,640]{3,2,1,0:T(8,128)S(1)}, u32[]{:S(2)}) copy-start(f32[4,24,96,640]{3,2,1,0:T(8,128)S(1)} %fusion.22) | copy-start | bytes 70778880
  464.4 4.6 copy-start.2
  469.0 1.7 copy-start.4
  469.0 1.7 copy-start.5
  470.7 34.7 %copy-start.1 = (bf16[128,640]{1,0:T(8,128)(2,1)S(1)}, bf16[128,640]{1,0:T(8,128)(2,1)}, u32[]{:S(2)}) copy-start(bf16[128,640]{1,0:T(8,128)(2,1)} %param.6) | copy-start | bytes 491524
Sparse Core Ops, SparseCore 0:
  32.1 321.7 all-gather.1
where the time goes:
time: 521 us; the launch traced here: 513 us
  blocking collectives  324 us (62%)
  local copies, waits for them, and re-layouts  119 us (23%)
  matrix products  36.6 us (7%)
  other arithmetic  17.5 us (3%)
  between operations  15.9 us (3%)
    all_to_all x1, blocking collectives, per_device(): lax.all_to_all(left_rows, GX, split_axis=2, concat_axis=1, tiled=True)  188 us
    all_to_all x1, blocking collectives, from_everyone(): lax.all_to_all(jnp.broadcast_to(array[None], (size, *array.shape)), axis,...  109 us
    all_gather x1, local copies, waits for them, and re-layouts, per_device(): lax.all_gather(right_proj, GX, axis=1, tiled=True)  57.9 us
    psum x4, blocking collectives, by_axis(): array = lax.psum(array, axis)  27.6 us
    all_to_all x2, local copies, waits for them, and re-layouts, per_device(): lax.all_to_all(left_rows, GX, split_axis=2, concat_axis=1, tiled=True)  27.4 us
    dot_general x1, matrix products, per_device(): jnp.einsum('bkic,bkjc->bijc', left_turned, lax.all_gather(right_proj, GX,...  22.7 us
    reshape x1, local copies, waits for them, and re-layouts, in_order(): return jnp.moveaxis(parts, 0, dim).reshape(lengths)  13.8 us
  transfers between devices with their start and end apart: 1, of which 0 were waited for; matrix products, arithmetic and copies ran while one was open for 11% of the time, Pallas kernels for 0%

commit v1 on v0

v1 whole, which is shorter than its diff:
```python
import jax
import jax.numpy as jnp
from jax import lax
from jax.experimental import pallas as pl
from jax.experimental.pallas import tpu as pltpu
from jax.sharding import Mesh
from jax.sharding import PartitionSpec as P

AXES = ("gz", "gx_0", "gx_1", "gy")
GX = ("gx_0", "gx_1")
MESH_ID = pl.DeviceIdType.MESH
F32 = jnp.float32
BF16 = jnp.bfloat16
EPS = 1e-05


def dot(a, b, ca, cb):
    return lax.dot_general(a, b, (((ca,), (cb,)), ((), ())), preferred_element_type=F32)


def kernel(
    entries,
    lens, pair, w_in, w_out,
    updated, magnitude,
    s_l, s_r, d_l, d_r, turned, s_t, d_t, normed, gates, w_proj, w_gate, w_last, s_mag, d_mag,
    send_l, send_r, send_t, send_m, recv_l, recv_r, recv_t, recv_m,
):
    core, z, y, x = (lax.axis_index(a) for a in AXES)
    gx = z * 4 + y
    me = gx * 4 + x

    barrier = pltpu.get_barrier_semaphore()

    def greet(r, carry):
        other = lax.rem(core * 64 + me + r, 128)
        pl.semaphore_signal(
            barrier,
            inc=1,
            device_id=(other // 64, other // 16 % 4, other // 4 % 4, other % 4),
            device_id_type=MESH_ID,
        )
        return carry

    lax.fori_loop(1, 128, greet, 0)

    row2 = lax.broadcasted_iota(jnp.int32, (256, 128), 0)
    col2 = lax.broadcasted_iota(jnp.int32, (256, 128), 1)
    twice = (row2 // 2 == col2).astype(BF16)
    even = row2 % 2 == 0
    for kind in range(4):
        part = dot(twice, w_in[:, kind * 128 : (kind + 1) * 128], 1, 1)
        part = part * (0.5 if kind % 2 else 1.0)
        rows = pl.ds(kind * 256, 256)
        w_proj[rows, 0:128] = jnp.where(even, part, 0.0).astype(BF16)
        w_proj[rows, 128:256] = jnp.where(even, 0.0, part).astype(BF16)
    part = dot(twice, w_out[...], 1, 0)
    w_last[:, 0:128] = jnp.where(even, part, 0.0).astype(BF16)
    w_last[:, 128:256] = jnp.where(even, 0.0, part).astype(BF16)
    half_gate = w_in[:, 512:640] * 0.5
    nothing = jnp.zeros((128, 128), BF16)
    w_gate[0:128, 0:128] = half_gate.astype(BF16)
    w_gate[0:128, 128:256] = nothing
    w_gate[128:256, 0:128] = nothing
    w_gate[128:256, 128:256] = half_gate.astype(BF16)

    my_len = [lens[core * 4 + b] for b in range(4)]
    lane = lax.broadcasted_iota(jnp.int32, (8, 128), 1)
    sub = lax.broadcasted_iota(jnp.int32, (8, 128), 0)
    group = lane // 32
    len_lane = jnp.where(
        group == 0,
        my_len[0],
        jnp.where(group == 1, my_len[1], jnp.where(group == 2, my_len[2], my_len[3])),
    )
    s_l2 = s_l.reshape(36, 256, 128)
    s_r2 = s_r.reshape(36, 256, 128)
    d_l2 = d_l.reshape(24, 384, 128)
    d_r2 = d_r.reshape(24, 384, 128)
    d_t2 = d_t.reshape(36, 256, 128)

    def pair_rows(row, third):
        return jnp.concatenate(
            [pair[b, row, third * 32 : (third + 1) * 32, :] for b in range(4)], axis=0
        )

    def normalize(third):
        def body(q, carry):
            halves = []
            for parity in range(2):
                v = pair_rows(2 * q + parity, third).astype(F32)
                mean_value = jnp.sum(v, axis=1, keepdims=True) * (1.0 / 128)
                v = v - mean_value
                variance = jnp.sum(v * v, axis=1, keepdims=True) * (1.0 / 128)
                halves.append((v * lax.rsqrt(variance + EPS)).astype(BF16))
            normed[third * 12 + q] = jnp.concatenate(halves, axis=1)
            return carry

        lax.fori_loop(0, 12, body, 0)

    def project(third, first, store):
        def body(q, carry):
            out = dot(w_proj[first : first + 512, :], normed[third * 12 + q], 1, 1)
            i_lane = x * 96 + third * 32 + lane % 32
            k_sub = gx * 24 + 2 * q + sub % 2
            half_mask = jnp.where((i_lane < len_lane) & (k_sub < len_lane), 0.5, 0.0)
            value = out[0:256].reshape(32, 8, 128) * half_mask[None]
            gate = jnp.tanh(out[256:512]).reshape(32, 8, 128) + 1.0
            store[third * 12 + q] = (value * gate).reshape(256, 128).astype(BF16)
            return carry

        lax.fori_loop(0, 12, body, 0)

    def other_of(r):
        off = lax.rem(r * 27, 64)
        oz = lax.rem(z + off // 16, 4)
        oy = lax.rem(y + off // 4 % 4, 4)
        ox = lax.rem(x + off % 4, 4)
        return oz, oy, ox

    def send_part(third, source, target, send_sem, recv_sem):
        def body(r, carry):
            oz, oy, ox = other_of(r)
            channel = (oz * 16 + oy * 4 + ox) * 2
            for c in range(2):
                pltpu.make_async_remote_copy(
                    src_ref=source.at[third, :, channel + c],
                    dst_ref=target.at[c, third, x, pl.ds(gx * 12, 12)],
                    send_sem=send_sem,
                    recv_sem=recv_sem.at[third],
                    device_id=(core, oz, oy, ox),
                    device_id_type=MESH_ID,
                ).start()
            return carry

        lax.fori_loop(1, 64, body, 0)
        for c in range(2):
            target[c, third, x, pl.ds(gx * 12, 12)] = source[third, :, me * 2 + c]

    def wait_part(sem):
        part = d_t.at[0, :, pl.ds(0, 126)]
        pltpu.make_async_copy(part, part, sem).wait()

    for third in range(3):
        normalize(third)
        project(third, 0, s_l2)
        if third == 0:
            pl.semaphore_wait(barrier, 127)
        send_part(third, s_l, d_l, send_l, recv_l)
    for third in range(3):
        project(third, 512, s_r2)
        send_part(third, s_r, d_r, send_r, recv_r)

    def gate_body(third):
        def body(q, carry):
            out = dot(normed[third * 12 + q], w_gate[...], 1, 0)
            parts = []
            for b in range(4):
                j_row = x * 96 + third * 32 + lax.broadcasted_iota(jnp.int32, (32, 256), 0)
                i_lane = gx * 24 + 2 * q + lax.broadcasted_iota(jnp.int32, (32, 256), 1) // 128
                live = (j_row < my_len[b]) & (i_lane < my_len[b])
                half = out[b * 32 : (b + 1) * 32]
                parts.append(jnp.where(live, jnp.tanh(half) * 0.5 + 0.5, 0.0))
            gates[third * 12 + q] = jnp.concatenate(parts, axis=0)
            return carry

        lax.fori_loop(0, 12, body, 0)

    for third in range(3):
        gate_body(third)

    for third in range(3):
        wait_part(recv_l.at[third])

        def turn(n, carry):
            c = n // 4
            col = lax.rem(n, 4)
            block = d_l2[c * 12 + third * 4 + col]
            turned[n, third * 128 : (third + 1) * 128, :] = block.T
            return carry

        lax.fori_loop(0, 8, turn, 0)

    lane4 = lax.broadcasted_iota(jnp.int32, (32, 512), 1) % 128 // 32

    def multiply(third):
        def body(r, carry):
            block = lax.rem(z + r, 4)
            for c in range(2):
                right = jnp.concatenate(
                    [d_r2[c * 12 + third * 4 + col] for col in range(4)], axis=1
                )
                out = dot(turned[c * 4 + block], right, 1, 0)
                rows = []
                for t in range(3):
                    g = [out[t * 128 + b * 32 : t * 128 + (b + 1) * 32] for b in range(4)]
                    rows.append(
                        jnp.where(
                            lane4 == 0,
                            g[0],
                            jnp.where(lane4 == 1, g[1], jnp.where(lane4 == 2, g[2], g[3])),
                        )
                    )
                full = jnp.concatenate(rows, axis=0)
                for piece in range(4):
                    for col in range(4):
                        s_t[third, block * 4 + piece, col, :, c] = (
                            full[piece * 24 : (piece + 1) * 24, col * 128 : (col + 1) * 128]
                            .astype(BF16)
                            .reshape(12, 2, 128)
                        )

            def send_one(n, inner):
                oy = lax.rem(y + n // 4, 4)
                ox = lax.rem(x + n, 4)
                pltpu.make_async_remote_copy(
                    src_ref=s_t.at[third, block * 4 + oy, ox],
                    dst_ref=d_t.at[third, :, pl.ds(me * 2, 2)],
                    send_sem=send_t,
                    recv_sem=recv_t.at[third],
                    device_id=(core, block, oy, ox),
                    device_id_type=MESH_ID,
                ).start()
                return inner

            lax.fori_loop(jnp.where(r == 4, 1, 0), 16, send_one, 0)
            return carry

        lax.fori_loop(1, 5, body, 0)
        d_t[third, :, pl.ds(me * 2, 2)] = s_t[third, gx, x]

    def finish(third, total):
        def body(q, total):
            v = d_t2[third * 12 + q].astype(F32).reshape(32, 8, 128)

            def over_channels(array):
                s = jnp.sum(array, axis=0)
                s = s + pltpu.roll(s, 4, 0)
                s = s + pltpu.roll(s, 2, 0)
                return s * (1.0 / 128)

            v = v - over_channels(v)[None]
            v = v * lax.rsqrt(over_channels(v * v) + EPS)[None]
            out = dot(v.reshape(256, 128).astype(BF16), w_last[...], 0, 0)
            change = out * gates[third * 12 + q]
            for parity in range(2):
                new = pair_rows(2 * q + parity, third).astype(F32)
                new = (new + change[:, parity * 128 : (parity + 1) * 128]).astype(BF16)
                for b in range(4):
                    updated[b, 2 * q + parity, third * 32 : (third + 1) * 32, :] = new[
                        b * 32 : (b + 1) * 32
                    ]
                total = total + jnp.sum(jnp.abs(new.astype(F32)).reshape(16, 8, 128), axis=0)
            return total

        return lax.fori_loop(0, 12, body, total)

    for third in range(3):
        wait_part(recv_r.at[third])
        multiply(third)
    total = jnp.zeros((8, 128), F32)
    for third in range(3):
        wait_part(recv_t.at[third])
        total = finish(third, total)

    flat = core * 64 + me
    s_mag[...] = jnp.sum(total, axis=0, keepdims=True)
    d_mag[flat] = jnp.sum(total, axis=0, keepdims=True)

    def tell(r, carry):
        other = lax.rem(flat + r, 128)
        pltpu.make_async_remote_copy(
            src_ref=s_mag,
            dst_ref=d_mag.at[flat],
            send_sem=send_m,
            recv_sem=recv_m,
            device_id=(other // 64, other // 16 % 4, other // 4 % 4, other % 4),
            device_id_type=MESH_ID,
        ).start()
        return carry

    lax.fori_loop(1, 128, tell, 0)
    for _ in range(3):
        wait_part(send_l)
        wait_part(send_r)
        wait_part(send_t)
    rest = d_mag.at[pl.ds(0, 127)]
    pltpu.make_async_copy(rest, rest, send_m).wait()
    pltpu.make_async_copy(rest, rest, recv_m).wait()
    everyone = jnp.sum(d_mag[...], axis=0)
    magnitude[...] = jnp.sum(everyone, axis=1, keepdims=True) * (1.0 / entries)


def per_device(entries, pair_repr, seq_lengths, weight_in, weight_out):
    vmem = pl.BlockSpec(memory_space=pltpu.VMEM)
    dma = pltpu.SemaphoreType.DMA
    updated, magnitude = pl.pallas_call(
        lambda *refs: kernel(entries, *refs),
        out_shape=(
            jax.ShapeDtypeStruct(pair_repr.shape, BF16),
            jax.ShapeDtypeStruct((1, 1), F32),
        ),
        in_specs=[pl.BlockSpec(memory_space=pltpu.SMEM), vmem, vmem, vmem],
        out_specs=(vmem, vmem),
        scratch_shapes=[
            pltpu.VMEM((3, 12, 128, 2, 128), BF16),
            pltpu.VMEM((3, 12, 128, 2, 128), BF16),
            pltpu.VMEM((2, 3, 4, 192, 2, 128), BF16),
            pltpu.VMEM((2, 3, 4, 192, 2, 128), BF16),
            pltpu.VMEM((8, 384, 384), BF16),
            pltpu.VMEM((3, 16, 4, 12, 2, 2, 128), BF16),
            pltpu.VMEM((3, 12, 128, 2, 128), BF16),
            pltpu.VMEM((36, 128, 256), BF16),
            pltpu.VMEM((36, 128, 256), F32),
            pltpu.VMEM((1024, 256), BF16),
            pltpu.VMEM((256, 256), BF16),
            pltpu.VMEM((256, 256), BF16),
            pltpu.VMEM((1, 128), F32),
            pltpu.VMEM((128, 1, 128), F32),
            dma,
            dma,
            dma,
            dma,
            dma((3,)),
            dma((3,)),
            dma((3,)),
            dma,
        ],
        compiler_params=pltpu.CompilerParams(
            collective_id=0, has_side_effects=True, vmem_limit_bytes=56 * 2**20
        ),
        name="triangle",
    )(seq_lengths, pair_repr, weight_in, weight_out)
    return updated, magnitude.reshape(())


def solution(mesh):
    finer = Mesh(mesh.devices.reshape(mesh.shape["gz"], 4, 4, mesh.shape["gy"]), AXES)
    entries = float(8 * 384 * 384 * 128)
    return jax.shard_map(
        lambda *args: per_device(entries, *args),
        mesh=finer,
        in_specs=(P("gz", GX, "gy", None), P(), P(), P()),
        out_specs=(P("gz", GX, "gy", None), P()),
        check_vma=False,
    )
```

time: 521 us -> 127 us (0.24); the launches traced: 513 us -> 126 us
  blocking collectives: 324 us -> 0 us
  Pallas kernels: 0 us -> 120 us
  local copies, waits for them, and re-layouts: 119 us -> 3.22 us
  matrix products: 36.6 us -> 0 us
  other arithmetic: 17.5 us -> 0 us
  between operations: 15.9 us -> 2.39 us
    all_to_all x2 -> x0, blocking collectives: 297 us -> none  [the longest x1 188 us: per_device(): lax.all_to_all(left_rows, GX, split_axis=2, concat_axis=1, tiled=True)]
    pallas_call x0 -> x1, Pallas kernels: none -> 120 us  [per_device(): pl.pallas_call(lambda *refs: kernel(entries, *refs), out_shape=(jax.Shape...]
    all_gather x1 -> x0, local copies, waits for them, and re-layouts: 57.9 us -> none  [per_device(): lax.all_gather(right_proj, GX, axis=1, tiled=True)]
    all_to_all x3 -> x0, local copies, waits for them, and re-layouts: 37.8 us -> none  [the longest x2 27.4 us: per_device(): lax.all_to_all(left_rows, GX, split_axis=2, concat_axis=1, tiled=True)]
    dot_general x3 -> x0, matrix products: 36.6 us -> none  [the longest x1 22.7 us: per_device(): jnp.einsum('bkic,bkjc->bijc', left_turned, lax.all_gather(right_proj, GX,...]
    psum x4 -> x0, blocking collectives: 27.6 us -> none  [by_axis(): array = lax.psum(array, axis)]
    reshape x1 -> x0, local copies, waits for them, and re-layouts: 13.8 us -> none  [in_order(): return jnp.moveaxis(parts, 0, dim).reshape(lengths)]
    reduce_sum x3 -> x0, other arithmetic: 10.7 us -> none  [the longest x2 8.12 us: layer_norm(): variance = jnp.mean(centered * centered, axis=-1, keepdims=True)]
  transfers between devices with their start and end apart: 1 -> 0, of which waited for: 0 -> 0; matrix products, arithmetic and copies ran while one was open for 11% -> 0% of each run, Pallas kernels for 0% -> 0%
where the time goes in v1:
time: 127 us; the launch traced here: 126 us
  Pallas kernels  120 us (94%)
  local copies, waits for them, and re-layouts  3.22 us (3%)
  between operations  2.39 us (2%)
    pallas_call x1, Pallas kernels, per_device(): pl.pallas_call(lambda *refs: kernel(entries, *refs), out_shape=(jax.Shape...  120 us
    unnamed x1, local copies, waits for them, and re-layouts  3.22 us

profile of v1, /device:TPU:1, one launch (start us, length us, event | category | flops | bytes accessed | tf_op | source)
XLA Modules:
  0.0 125.6 jit_solution(5791232308874045934)
XLA Ops:
  0.6 120.0 %triangle.1 = (bf16[4,24,96,128]{3,2,1,0:T(8,128)(2,1)}, f32[1,1]{1,0:T(1,128)}) custom-call(s32[8]{0:T(128)} %refs_0_.1, bf16[4,24,96,128]{3,2,1,0:T(8,128)(2,1)} %refs_1_.1, bf16[128,640]{1,0:T(8,128)(2,1)} %refs_2_.1, bf16[128,128]{1,0:T(8,128)(2,1)} %refs_3_.1), custom_call_target="tpu_custom_call" | custom-call | tf_op jit(solution)/shard_map/triangle/pallas_call | solution.py:296
  120.6 3.2 %copy.8 = bf16[4,24,96,128]{3,2,1,0:T(8,128)(2,1)} copy(bf16[4,24,96,128]{3,2,1,0:T(8,128)(2,1)} %get-tuple-element.8) | data formatting | bytes 4718592

commit v2 on v1

--- a/solution.py
+++ b/solution.py
@@ -12,6 +12,19 @@
 F32 = jnp.float32
 BF16 = jnp.bfloat16
 EPS = 1e-05
+U_NORM = 3
+U_PROJ = 2
+U_GATE = 2
+U_LAST = 2
+
+
+def steps(count, unroll, body, carry):
+    def several(n, carry):
+        for u in range(unroll):
+            carry = body(n * unroll + u, carry)
+        return carry
+
+    return lax.fori_loop(0, count // unroll, several, carry)
 
 
 def dot(a, b, ca, cb):
@@ -20,48 +33,63 @@
 
 def kernel(
     entries,
-    lens, pair, w_in, w_out,
+    lens, pair_hbm, w_in_hbm, w_out_hbm,
     updated, magnitude,
-    s_l, s_r, d_l, d_r, turned, s_t, d_t, normed, gates, w_proj, w_gate, w_last, s_mag, d_mag,
-    send_l, send_r, send_t, send_m, recv_l, recv_r, recv_t, recv_m,
+    pair, w_in, w_out,
+    s_l, s_r, d_l, d_r, turned, s_t, d_t, normed, gates, w_proj, w_gate, w_last,
+    s_plane, d_plane, s_all, d_all,
+    send_l, send_r, send_t, send_m, recv_l, recv_r, recv_t, recv_plane, recv_all,
+    fetched,
 ):
     core, z, y, x = (lax.axis_index(a) for a in AXES)
     gx = z * 4 + y
     me = gx * 4 + x
 
+    def columns(third):
+        return pl.ds(third * 32, 32)
+
+    fetch = [
+        pltpu.make_async_copy(w_in_hbm, w_in, fetched.at[3]),
+        pltpu.make_async_copy(
+            pair_hbm.at[:, :, columns(0)], pair.at[:, :, columns(0)], fetched.at[0]
+        ),
+        pltpu.make_async_copy(w_out_hbm, w_out, fetched.at[4]),
+        pltpu.make_async_copy(
+            pair_hbm.at[:, :, columns(1)], pair.at[:, :, columns(1)], fetched.at[1]
+        ),
+        pltpu.make_async_copy(
+            pair_hbm.at[:, :, columns(2)], pair.at[:, :, columns(2)], fetched.at[2]
+        ),
+    ]
+    for copy in fetch:
+        copy.start()
+
     barrier = pltpu.get_barrier_semaphore()
-
-    def greet(r, carry):
-        other = lax.rem(core * 64 + me + r, 128)
-        pl.semaphore_signal(
-            barrier,
-            inc=1,
-            device_id=(other // 64, other // 16 % 4, other // 4 % 4, other % 4),
-            device_id_type=MESH_ID,
-        )
-        return carry
-
-    lax.fori_loop(1, 128, greet, 0)
+    zs = [lax.rem(z + n, 4) for n in range(4)]
+    ys = [lax.rem(y + n, 4) for n in range(4)]
+    xs = [lax.rem(x + n, 4) for n in range(4)]
+
+    def greet(device):
+        pl.semaphore_signal(barrier, inc=1, device_id=device, device_id_type=MESH_ID)
+
+    for dz in range(4):
+        for dy in range(4):
+            for dx in range(4):
+                if dz or dy or dx:
+                    greet((core, zs[dz], ys[dy], xs[dx]))
+        greet((1 - core, zs[dz], y, x))
 
     row2 = lax.broadcasted_iota(jnp.int32, (256, 128), 0)
     col2 = lax.broadcasted_iota(jnp.int32, (256, 128), 1)
     twice = (row2 // 2 == col2).astype(BF16)
     even = row2 % 2 == 0
+    fetch[0].wait()
     for kind in range(4):
         part = dot(twice, w_in[:, kind * 128 : (kind + 1) * 128], 1, 1)
         part = part * (0.5 if kind % 2 else 1.0)
         rows = pl.ds(kind * 256, 256)
         w_proj[rows, 0:128] = jnp.where(even, part, 0.0).astype(BF16)
         w_proj[rows, 128:256] = jnp.where(even, 0.0, part).astype(BF16)
-    part = dot(twice, w_out[...], 1, 0)
-    w_last[:, 0:128] = jnp.where(even, part, 0.0).astype(BF16)
-    w_last[:, 128:256] = jnp.where(even, 0.0, part).astype(BF16)
-    half_gate = w_in[:, 512:640] * 0.5
-    nothing = jnp.zeros((128, 128), BF16)
-    w_gate[0:128, 0:128] = half_gate.astype(BF16)
-    w_gate[0:128, 128:256] = nothing
-    w_gate[128:256, 0:128] = nothing
-    w_gate[128:256, 128:256] = half_gate.astype(BF16)
 
     my_len = [lens[core * 4 + b] for b in range(4)]
     lane = lax.broadcasted_iota(jnp.int32, (8, 128), 1)
@@ -95,7 +123,7 @@
             normed[third * 12 + q] = jnp.concatenate(halves, axis=1)
             return carry
 
-        lax.fori_loop(0, 12, body, 0)
+        steps(12, U_NORM, body, 0)
 
     def project(third, first, store):
         def body(q, carry):
@@ -108,18 +136,22 @@
             store[third * 12 + q] = (value * gate).reshape(256, 128).astype(BF16)
             return carry
 
-        lax.fori_loop(0, 12, body, 0)
-
-    def other_of(r):
-        off = lax.rem(r * 27, 64)
-        oz = lax.rem(z + off // 16, 4)
-        oy = lax.rem(y + off // 4 % 4, 4)
-        ox = lax.rem(x + off % 4, 4)
-        return oz, oy, ox
+        steps(12, U_PROJ, body, 0)
+
+    def to_others(send):
+        def body(n, carry):
+            oz = lax.rem(z + n, 4)
+            oy = lax.rem(y + n // 4, 4)
+            for dx in range(4):
+                send(lax.rem(oz + dx, 4), lax.rem(oy + dx, 4), xs[dx])
+            return carry
+
+        lax.fori_loop(1, 16, body, 0)
+        for dx in range(1, 4):
+            send(zs[dx], ys[dx], xs[dx])
 
     def send_part(third, source, target, send_sem, recv_sem):
-        def body(r, carry):
-            oz, oy, ox = other_of(r)
+        def send(oz, oy, ox):
             channel = (oz * 16 + oy * 4 + ox) * 2
             for c in range(2):
                 pltpu.make_async_remote_copy(
@@ -130,25 +162,36 @@
                     device_id=(core, oz, oy, ox),
                     device_id_type=MESH_ID,
                 ).start()
-            return carry
-
-        lax.fori_loop(1, 64, body, 0)
+
+        to_others(send)
         for c in range(2):
             target[c, third, x, pl.ds(gx * 12, 12)] = source[third, :, me * 2 + c]
 
-    def wait_part(sem):
-        part = d_t.at[0, :, pl.ds(0, 126)]
+    def wait_part(sem, rows=12):
+        part = d_t.at[0, pl.ds(0, rows), pl.ds(0, 126)]
         pltpu.make_async_copy(part, part, sem).wait()
 
     for third in range(3):
+        fetch[(1, 3, 4)[third]].wait()
         normalize(third)
         project(third, 0, s_l2)
         if third == 0:
-            pl.semaphore_wait(barrier, 127)
+            pl.semaphore_wait(barrier, 67)
         send_part(third, s_l, d_l, send_l, recv_l)
     for third in range(3):
         project(third, 512, s_r2)
         send_part(third, s_r, d_r, send_r, recv_r)
+
+    fetch[2].wait()
+    part = dot(twice, w_out[...], 1, 0)
+    w_last[:, 0:128] = jnp.where(even, part, 0.0).astype(BF16)
+    w_last[:, 128:256] = jnp.where(even, 0.0, part).astype(BF16)
+    half_gate = w_in[:, 512:640] * 0.5
+    nothing = jnp.zeros((128, 128), BF16)
+    w_gate[0:128, 0:128] = half_gate.astype(BF16)
+    w_gate[0:128, 128:256] = nothing
+    w_gate[128:256, 0:128] = nothing
+    w_gate[128:256, 128:256] = half_gate.astype(BF16)
 
     def gate_body(third):
         def body(q, carry):
@@ -163,7 +206,7 @@
             gates[third * 12 + q] = jnp.concatenate(parts, axis=0)
             return carry
 
-        lax.fori_loop(0, 12, body, 0)
+        steps(12, U_GATE, body, 0)
 
     for third in range(3):
         gate_body(third)
@@ -182,9 +225,10 @@
 
     lane4 = lax.broadcasted_iota(jnp.int32, (32, 512), 1) % 128 // 32
 
-    def multiply(third):
+    def multiply(third, after):
         def body(r, carry):
-            block = lax.rem(z + r, 4)
+            shift = lax.rem(r + 2 * core, 4)
+            block = lax.rem(z + shift, 4)
             for c in range(2):
                 right = jnp.concatenate(
                     [d_r2[c * 12 + third * 4 + col] for col in range(4)], axis=1
@@ -209,26 +253,40 @@
                             .reshape(12, 2, 128)
                         )
 
-            def send_one(n, inner):
-                oy = lax.rem(y + n // 4, 4)
-                ox = lax.rem(x + n, 4)
-                pltpu.make_async_remote_copy(
-                    src_ref=s_t.at[third, block * 4 + oy, ox],
-                    dst_ref=d_t.at[third, :, pl.ds(me * 2, 2)],
-                    send_sem=send_t,
-                    recv_sem=recv_t.at[third],
-                    device_id=(core, block, oy, ox),
-                    device_id_type=MESH_ID,
-                ).start()
-                return inner
-
-            lax.fori_loop(jnp.where(r == 4, 1, 0), 16, send_one, 0)
+            after(block, jnp.where(shift == 0, 1, 0))
             return carry
 
         lax.fori_loop(1, 5, body, 0)
         d_t[third, :, pl.ds(me * 2, 2)] = s_t[third, gx, x]
 
-    def finish(third, total):
+    def send_back(third, oz, oy, ox, first, count, sem):
+        pltpu.make_async_remote_copy(
+            src_ref=s_t.at[third, oz * 4 + oy, ox, pl.ds(first, count)],
+            dst_ref=d_t.at[third, pl.ds(first, count), pl.ds(me * 2, 2)],
+            send_sem=send_t,
+            recv_sem=sem,
+            device_id=(core, oz, oy, ox),
+            device_id_type=MESH_ID,
+        ).start()
+
+    def send_block(third, block, own, first, count, sem):
+        def body(n, carry):
+            for dx in range(4):
+                send_back(third, block, lax.rem(y + n + dx, 4), xs[dx], first, count, sem)
+            return carry
+
+        lax.fori_loop(1, 4, body, 0)
+        for dx in range(1, 4):
+            send_back(third, block, ys[dx], xs[dx], first, count, sem)
+
+        @pl.when(own == 0)
+        def _():
+            send_back(third, block, y, x, first, count, sem)
+
+    def send_third(third, first, count, sem):
+        to_others(lambda oz, oy, ox: send_back(third, oz, oy, ox, first, count, sem))
+
+    def finish(third, first, count, total):
         def body(q, total):
             v = d_t2[third * 12 + q].astype(F32).reshape(32, 8, 128)
 
@@ -252,56 +310,87 @@
                 total = total + jnp.sum(jnp.abs(new.astype(F32)).reshape(16, 8, 128), axis=0)
             return total
 
-        return lax.fori_loop(0, 12, body, total)
-
-    for third in range(3):
-        wait_part(recv_r.at[third])
-        multiply(third)
+        return steps(count, U_LAST, lambda n, carry: body(first + n, carry), total)
+
+    def hold(block, own):
+        pass
+
+    wait_part(recv_r.at[0])
+    multiply(0, hold)
+    wait_part(recv_r.at[1])
+    send_third(0, 0, 12, recv_t.at[0])
+    multiply(1, hold)
+    wait_part(recv_r.at[2])
+    send_third(1, 0, 12, recv_t.at[1])
+    multiply(2, lambda block, own: send_block(2, block, own, 0, 6, recv_t.at[2]))
+    send_third(2, 6, 6, recv_t.at[3])
     total = jnp.zeros((8, 128), F32)
-    for third in range(3):
+    for third in range(2):
         wait_part(recv_t.at[third])
-        total = finish(third, total)
-
-    flat = core * 64 + me
-    s_mag[...] = jnp.sum(total, axis=0, keepdims=True)
-    d_mag[flat] = jnp.sum(total, axis=0, keepdims=True)
-
-    def tell(r, carry):
-        other = lax.rem(flat + r, 128)
-        pltpu.make_async_remote_copy(
-            src_ref=s_mag,
-            dst_ref=d_mag.at[flat],
-            send_sem=send_m,
-            recv_sem=recv_m,
-            device_id=(other // 64, other // 16 % 4, other // 4 % 4, other % 4),
-            device_id_type=MESH_ID,
-        ).start()
-        return carry
-
-    lax.fori_loop(1, 128, tell, 0)
+        total = finish(third, 0, 12, total)
+    wait_part(recv_t.at[2], 6)
+    total = finish(2, 0, 6, total)
+    wait_part(recv_t.at[3], 6)
+    total = finish(2, 6, 6, total)
+    mine = jnp.sum(total, axis=0, keepdims=True)
+    s_plane[...] = mine
+    d_plane[y * 4 + x] = mine
     for _ in range(3):
         wait_part(send_l)
         wait_part(send_r)
         wait_part(send_t)
-    rest = d_mag.at[pl.ds(0, 127)]
+
+    for dy in range(4):
+        for dx in range(4):
+            if dy or dx:
+                pltpu.make_async_remote_copy(
+                    src_ref=s_plane,
+                    dst_ref=d_plane.at[y * 4 + x],
+                    send_sem=send_m,
+                    recv_sem=recv_plane,
+                    device_id=(core, z, ys[dy], xs[dx]),
+                    device_id_type=MESH_ID,
+                ).start()
+    rest = d_plane.at[pl.ds(0, 15)]
+    pltpu.make_async_copy(rest, rest, recv_plane).wait()
+    plane = jnp.sum(d_plane[...], axis=0)
+    s_all[...] = plane
+    d_all[core * 4 + z] = plane
     pltpu.make_async_copy(rest, rest, send_m).wait()
-    pltpu.make_async_copy(rest, rest, recv_m).wait()
-    everyone = jnp.sum(d_mag[...], axis=0)
+    for dz in range(4):
+        for other_core in (core, 1 - core):
+            if dz or other_core is not core:
+                pltpu.make_async_remote_copy(
+                    src_ref=s_all,
+                    dst_ref=d_all.at[core * 4 + z],
+                    send_sem=send_m,
+                    recv_sem=recv_all,
+                    device_id=(other_core, zs[dz], y, x),
+                    device_id_type=MESH_ID,
+                ).start()
+    rest = d_all.at[pl.ds(0, 7)]
+    pltpu.make_async_copy(rest, rest, recv_all).wait()
+    everyone = jnp.sum(d_all[...], axis=0)
     magnitude[...] = jnp.sum(everyone, axis=1, keepdims=True) * (1.0 / entries)
+    pltpu.make_async_copy(rest, rest, send_m).wait()
 
 
 def per_device(entries, pair_repr, seq_lengths, weight_in, weight_out):
     vmem = pl.BlockSpec(memory_space=pltpu.VMEM)
+    hbm = pl.BlockSpec(memory_space=pl.ANY)
     dma = pltpu.SemaphoreType.DMA
     updated, magnitude = pl.pallas_call(
         lambda *refs: kernel(entries, *refs),
         out_shape=(
-            jax.ShapeDtypeStruct(pair_repr.shape, BF16),
+            pltpu.VMEM(pair_repr.shape, BF16),
             jax.ShapeDtypeStruct((1, 1), F32),
         ),
-        in_specs=[pl.BlockSpec(memory_space=pltpu.SMEM), vmem, vmem, vmem],
+        in_specs=[pl.BlockSpec(memory_space=pltpu.SMEM), hbm, hbm, hbm],
         out_specs=(vmem, vmem),
         scratch_shapes=[
+            pltpu.VMEM(pair_repr.shape, BF16),
+            pltpu.VMEM(weight_in.shape, BF16),
+            pltpu.VMEM(weight_out.shape, BF16),
             pltpu.VMEM((3, 12, 128, 2, 128), BF16),
             pltpu.VMEM((3, 12, 128, 2, 128), BF16),
             pltpu.VMEM((2, 3, 4, 192, 2, 128), BF16),
@@ -315,15 +404,19 @@
             pltpu.VMEM((256, 256), BF16),
             pltpu.VMEM((256, 256), BF16),
             pltpu.VMEM((1, 128), F32),
-            pltpu.VMEM((128, 1, 128), F32),
+            pltpu.VMEM((16, 1, 128), F32),
+            pltpu.VMEM((1, 128), F32),
+            pltpu.VMEM((8, 1, 128), F32),
             dma,
             dma,
             dma,
             dma,
             dma((3,)),
             dma((3,)),
-            dma((3,)),
-            dma,
+            dma((4,)),
+            dma,
+            dma,
+            dma((5,)),
         ],
         compiler_params=pltpu.CompilerParams(
             collective_id=0, has_side_effects=True, vmem_limit_bytes=56 * 2**20

time: 127 us -> 108 us (0.85); the launches traced: 126 us -> 108 us
  Pallas kernels: 120 us -> 104 us
  local copies, waits for them, and re-layouts: 3.22 us -> 1.41 us
    pallas_call x1, Pallas kernels: 120 us -> 104 us  [per_device(): pl.pallas_call(lambda *refs: kernel(entries, *refs), out_shape=(pltpu.VME...]
    unnamed x1, local copies, waits for them, and re-layouts: 3.22 us -> 1.41 us
where the time goes in v2:
time: 108 us
  Pallas kernels  104 us (96%)
  between operations  2.33 us (2%)
  local copies, waits for them, and re-layouts  1.41 us (1%)
    pallas_call x1, Pallas kernels, per_device(): pl.pallas_call(lambda *refs: kernel(entries, *refs), out_shape=(pltpu.VME...  104 us

profile of v2, /device:TPU:1, one launch (start us, length us, event | category | flops | bytes accessed | tf_op | source)
XLA Modules:
  0.0 108.1 jit_solution(11957032277133043627)
XLA Ops:
  0.6 104.4 %triangle.1 = (bf16[4,24,96,128]{3,2,1,0:T(8,128)(2,1)S(1)}, f32[1,1]{1,0:T(1,128)}) custom-call(s32[8]{0:T(128)} %refs_0_.1, bf16[4,24,96,128]{3,2,1,0:T(8,128)(2,1)} %refs_1_.1, bf16[128,640]{1,0:T(8,128)(2,1)} %refs_2_.1, bf16[128,128]{1,0:T(8,128)(2,1)} %refs_3_.1), custom_call_target="tpu_custom_call" | custom-call | tf_op jit(solution)/shard_map/triangle/pallas_call | solution.py:382
  105.0 1.4 %copy.8 = bf16[4,24,96,128]{3,2,1,0:T(8,128)(2,1)} copy(bf16[4,24,96,128]{3,2,1,0:T(8,128)(2,1)S(1)} %get-tuple-element.6) | data formatting | bytes 4718592

commit v3 on v2

--- a/solution.py
+++ b/solution.py
@@ -15,7 +15,7 @@
 U_NORM = 3
 U_PROJ = 2
 U_GATE = 2
-U_LAST = 2
+U_LAST = 3
 
 
 def steps(count, unroll, body, carry):
@@ -37,22 +37,36 @@
     updated, magnitude,
     pair, w_in, w_out,
     s_l, s_r, d_l, d_r, turned, s_t, d_t, normed, gates, w_proj, w_gate, w_last,
-    s_plane, d_plane, s_all, d_all,
-    send_l, send_r, send_t, send_m, recv_l, recv_r, recv_t, recv_plane, recv_all,
-    fetched,
+    s_all, d_all,
+    send_l, send_r, send_t, send_m, recv_l, recv_r, recv_t, recv_all,
+    fetched, slab,
 ):
     core, z, y, x = (lax.axis_index(a) for a in AXES)
     gx = z * 4 + y
     me = gx * 4 + x
 
+    barrier = pltpu.get_barrier_semaphore()
+    zs = [lax.rem(z + n, 4) for n in range(4)]
+    ys = [lax.rem(y + n, 4) for n in range(4)]
+    xs = [lax.rem(x + n, 4) for n in range(4)]
+    cores = [core, 1 - core]
+    far_first = sorted(
+        ((dc, dz, dy, dx) for dc in range(2) for dz in range(4) for dy in range(4) for dx in range(4)),
+        key=lambda d: -sum(min(n, 4 - n) for n in d[1:]),
+    )[:-2] + [(1, 0, 0, 0)]
+    everyone_else = [(cores[dc], zs[dz], ys[dy], xs[dx]) for dc, dz, dy, dx in far_first]
+    for device, step in zip(everyone_else, far_first):
+        if step[0] == 0 or step == (1, 0, 0, 0):
+            pl.semaphore_signal(barrier, inc=1, device_id=device, device_id_type=MESH_ID)
+
     def columns(third):
         return pl.ds(third * 32, 32)
 
     fetch = [
-        pltpu.make_async_copy(w_in_hbm, w_in, fetched.at[3]),
         pltpu.make_async_copy(
             pair_hbm.at[:, :, columns(0)], pair.at[:, :, columns(0)], fetched.at[0]
         ),
+        pltpu.make_async_copy(w_in_hbm, w_in, fetched.at[3]),
         pltpu.make_async_copy(w_out_hbm, w_out, fetched.at[4]),
         pltpu.make_async_copy(
             pair_hbm.at[:, :, columns(1)], pair.at[:, :, columns(1)], fetched.at[1]
@@ -64,32 +78,18 @@
     for copy in fetch:
         copy.start()
 
-    barrier = pltpu.get_barrier_semaphore()
-    zs = [lax.rem(z + n, 4) for n in range(4)]
-    ys = [lax.rem(y + n, 4) for n in range(4)]
-    xs = [lax.rem(x + n, 4) for n in range(4)]
-
-    def greet(device):
-        pl.semaphore_signal(barrier, inc=1, device_id=device, device_id_type=MESH_ID)
-
-    for dz in range(4):
-        for dy in range(4):
-            for dx in range(4):
-                if dz or dy or dx:
-                    greet((core, zs[dz], ys[dy], xs[dx]))
-        greet((1 - core, zs[dz], y, x))
-
     row2 = lax.broadcasted_iota(jnp.int32, (256, 128), 0)
     col2 = lax.broadcasted_iota(jnp.int32, (256, 128), 1)
     twice = (row2 // 2 == col2).astype(BF16)
     even = row2 % 2 == 0
-    fetch[0].wait()
-    for kind in range(4):
-        part = dot(twice, w_in[:, kind * 128 : (kind + 1) * 128], 1, 1)
-        part = part * (0.5 if kind % 2 else 1.0)
-        rows = pl.ds(kind * 256, 256)
-        w_proj[rows, 0:128] = jnp.where(even, part, 0.0).astype(BF16)
-        w_proj[rows, 128:256] = jnp.where(even, 0.0, part).astype(BF16)
+    def prepare():
+        fetch[1].wait()
+        for kind in range(4):
+            part = dot(twice, w_in[:, kind * 128 : (kind + 1) * 128], 1, 1)
+            part = part * (0.5 if kind % 2 else 1.0)
+            rows = pl.ds(kind * 256, 256)
+            w_proj[rows, 0:128] = jnp.where(even, part, 0.0).astype(BF16)
+            w_proj[rows, 128:256] = jnp.where(even, 0.0, part).astype(BF16)
 
     my_len = [lens[core * 4 + b] for b in range(4)]
     lane = lax.broadcasted_iota(jnp.int32, (8, 128), 1)
@@ -111,8 +111,9 @@
             [pair[b, row, third * 32 : (third + 1) * 32, :] for b in range(4)], axis=0
         )
 
-    def normalize(third):
-        def body(q, carry):
+    def normalize(third, first, count):
+        def body(n, carry):
+            q = first + n
             halves = []
             for parity in range(2):
                 v = pair_rows(2 * q + parity, third).astype(F32)
@@ -123,11 +124,12 @@
             normed[third * 12 + q] = jnp.concatenate(halves, axis=1)
             return carry
 
-        steps(12, U_NORM, body, 0)
-
-    def project(third, first, store):
-        def body(q, carry):
-            out = dot(w_proj[first : first + 512, :], normed[third * 12 + q], 1, 1)
+        steps(count, U_NORM, body, 0)
+
+    def project(third, first, count, row, store):
+        def body(n, carry):
+            q = first + n
+            out = dot(w_proj[row : row + 512, :], normed[third * 12 + q], 1, 1)
             i_lane = x * 96 + third * 32 + lane % 32
             k_sub = gx * 24 + 2 * q + sub % 2
             half_mask = jnp.where((i_lane < len_lane) & (k_sub < len_lane), 0.5, 0.0)
@@ -136,7 +138,7 @@
             store[third * 12 + q] = (value * gate).reshape(256, 128).astype(BF16)
             return carry
 
-        steps(12, U_PROJ, body, 0)
+        steps(count, U_PROJ, body, 0)
 
     def to_others(send):
         def body(n, carry):
@@ -150,13 +152,13 @@
         for dx in range(1, 4):
             send(zs[dx], ys[dx], xs[dx])
 
-    def send_part(third, source, target, send_sem, recv_sem):
+    def send_part(third, first, count, source, target, send_sem, recv_sem):
         def send(oz, oy, ox):
             channel = (oz * 16 + oy * 4 + ox) * 2
             for c in range(2):
                 pltpu.make_async_remote_copy(
-                    src_ref=source.at[third, :, channel + c],
-                    dst_ref=target.at[c, third, x, pl.ds(gx * 12, 12)],
+                    src_ref=source.at[third, pl.ds(first, count), channel + c],
+                    dst_ref=target.at[c, third, x, pl.ds(gx * 12 + first, count)],
                     send_sem=send_sem,
                     recv_sem=recv_sem.at[third],
                     device_id=(core, oz, oy, ox),
@@ -165,22 +167,30 @@
 
         to_others(send)
         for c in range(2):
-            target[c, third, x, pl.ds(gx * 12, 12)] = source[third, :, me * 2 + c]
+            target[c, third, x, pl.ds(gx * 12 + first, count)] = source[
+                third, first : first + count, me * 2 + c
+            ]
 
     def wait_part(sem, rows=12):
         part = d_t.at[0, pl.ds(0, rows), pl.ds(0, 126)]
         pltpu.make_async_copy(part, part, sem).wait()
 
     for third in range(3):
-        fetch[(1, 3, 4)[third]].wait()
-        normalize(third)
-        project(third, 0, s_l2)
-        if third == 0:
-            pl.semaphore_wait(barrier, 67)
-        send_part(third, s_l, d_l, send_l, recv_l)
+        fetch[(0, 3, 4)[third]].wait()
+        for first, count in ((0, 6), (6, 6)) if third == 0 else ((0, 12),):
+            normalize(third, first, count)
+            if third == 0 and first == 0:
+                prepare()
+            project(third, first, count, 0, s_l2)
+            if third == 0 and first == 0:
+                pl.semaphore_wait(barrier, 64)
+                pl.semaphore_signal(
+                    slab, inc=1, device_id=(1 - core, z, y, x), device_id_type=MESH_ID
+                )
+            send_part(third, first, count, s_l, d_l, send_l, recv_l)
     for third in range(3):
-        project(third, 512, s_r2)
-        send_part(third, s_r, d_r, send_r, recv_r)
+        project(third, 0, 12, 512, s_r2)
+        send_part(third, 0, 12, s_r, d_r, send_r, recv_r)
 
     fetch[2].wait()
     part = dot(twice, w_out[...], 1, 0)
@@ -310,7 +320,7 @@
                 total = total + jnp.sum(jnp.abs(new.astype(F32)).reshape(16, 8, 128), axis=0)
             return total
 
-        return steps(count, U_LAST, lambda n, carry: body(first + n, carry), total)
+        return steps(count, 3 if count == 3 else U_LAST, lambda n, carry: body(first + n, carry), total)
 
     def hold(block, own):
         pass
@@ -318,8 +328,8 @@
     wait_part(recv_r.at[0])
     multiply(0, hold)
     wait_part(recv_r.at[1])
+    multiply(1, hold)
     send_third(0, 0, 12, recv_t.at[0])
-    multiply(1, hold)
     wait_part(recv_r.at[2])
     send_third(1, 0, 12, recv_t.at[1])
     multiply(2, lambda block, own: send_block(2, block, own, 0, 6, recv_t.at[2]))
@@ -332,45 +342,28 @@
     total = finish(2, 0, 6, total)
     wait_part(recv_t.at[3], 6)
     total = finish(2, 6, 6, total)
+
+    flat = core * 64 + me
     mine = jnp.sum(total, axis=0, keepdims=True)
-    s_plane[...] = mine
-    d_plane[y * 4 + x] = mine
+    s_all[...] = mine
+    d_all[flat] = mine
     for _ in range(3):
         wait_part(send_l)
         wait_part(send_r)
         wait_part(send_t)
-
-    for dy in range(4):
-        for dx in range(4):
-            if dy or dx:
-                pltpu.make_async_remote_copy(
-                    src_ref=s_plane,
-                    dst_ref=d_plane.at[y * 4 + x],
-                    send_sem=send_m,
-                    recv_sem=recv_plane,
-                    device_id=(core, z, ys[dy], xs[dx]),
-                    device_id_type=MESH_ID,
-                ).start()
-    rest = d_plane.at[pl.ds(0, 15)]
-    pltpu.make_async_copy(rest, rest, recv_plane).wait()
-    plane = jnp.sum(d_plane[...], axis=0)
-    s_all[...] = plane
-    d_all[core * 4 + z] = plane
-    pltpu.make_async_copy(rest, rest, send_m).wait()
-    for dz in range(4):
-        for other_core in (core, 1 - core):
-            if dz or other_core is not core:
-                pltpu.make_async_remote_copy(
-                    src_ref=s_all,
-                    dst_ref=d_all.at[core * 4 + z],
-                    send_sem=send_m,
-                    recv_sem=recv_all,
-                    device_id=(other_core, zs[dz], y, x),
-                    device_id_type=MESH_ID,
-                ).start()
-    rest = d_all.at[pl.ds(0, 7)]
+    pl.semaphore_wait(slab, 1)
+    for device in everyone_else:
+        pltpu.make_async_remote_copy(
+            src_ref=s_all,
+            dst_ref=d_all.at[flat],
+            send_sem=send_m,
+            recv_sem=recv_all,
+            device_id=device,
+            device_id_type=MESH_ID,
+        ).start()
+    rest = d_all.at[pl.ds(0, 127)]
     pltpu.make_async_copy(rest, rest, recv_all).wait()
-    everyone = jnp.sum(d_all[...], axis=0)
+    everyone = jnp.sum(d_all.reshape(128, 128)[...], axis=0, keepdims=True)
     magnitude[...] = jnp.sum(everyone, axis=1, keepdims=True) * (1.0 / entries)
     pltpu.make_async_copy(rest, rest, send_m).wait()
 
@@ -404,19 +397,17 @@
             pltpu.VMEM((256, 256), BF16),
             pltpu.VMEM((256, 256), BF16),
             pltpu.VMEM((1, 128), F32),
-            pltpu.VMEM((16, 1, 128), F32),
-            pltpu.VMEM((1, 128), F32),
-            pltpu.VMEM((8, 1, 128), F32),
+            pltpu.VMEM((128, 1, 128), F32),
             dma,
             dma,
             dma,
             dma,
             dma((3,)),
             dma((3,)),
-            dma((4,)),
-            dma,
+            dma((5,)),
             dma,
             dma((5,)),
+            pltpu.SemaphoreType.REGULAR,
         ],
         compiler_params=pltpu.CompilerParams(
             collective_id=0, has_side_effects=True, vmem_limit_bytes=56 * 2**20

time: 108 us -> 105 us (0.972)
  Pallas kernels: 104 us -> 101 us
    pallas_call x1, Pallas kernels: 104 us -> 101 us  [per_device(): pl.pallas_call(lambda *refs: kernel(entries, *refs), out_shape=(pltpu.VME...]
where the time goes in v3:
time: 105 us
  Pallas kernels  101 us (96%)
  between operations  2.33 us (2%)
  local copies, waits for them, and re-layouts  1.41 us (1%)
    pallas_call x1, Pallas kernels, per_device(): pl.pallas_call(lambda *refs: kernel(entries, *refs), out_shape=(pltpu.VME...  101 us

profile of v3, /device:TPU:1, one launch (start us, length us, event | category | flops | bytes accessed | tf_op | source)
XLA Modules:
  0.0 104.6 jit_solution(15650812391209203245)
XLA Ops:
  0.6 100.9 %triangle.1 = (bf16[4,24,96,128]{3,2,1,0:T(8,128)(2,1)S(1)}, f32[1,1]{1,0:T(1,128)}) custom-call(s32[8]{0:T(128)} %refs_0_.1, bf16[4,24,96,128]{3,2,1,0:T(8,128)(2,1)} %refs_1_.1, bf16[128,640]{1,0:T(8,128)(2,1)} %refs_2_.1, bf16[128,128]{1,0:T(8,128)(2,1)} %refs_3_.1), custom_call_target="tpu_custom_call" | custom-call | tf_op jit(solution)/shard_map/triangle/pallas_call | solution.py:375
  101.5 1.4 %copy.8 = bf16[4,24,96,128]{3,2,1,0:T(8,128)(2,1)} copy(bf16[4,24,96,128]{3,2,1,0:T(8,128)(2,1)S(1)} %get-tuple-element.6) | data formatting | bytes 4718592

commit v4 on v3

--- a/solution.py
+++ b/solution.py
@@ -15,7 +15,7 @@
 U_NORM = 3
 U_PROJ = 2
 U_GATE = 2
-U_LAST = 3
+U_LAST = 6
 
 
 def steps(count, unroll, body, carry):
@@ -33,10 +33,10 @@
 
 def kernel(
     entries,
-    lens, pair_hbm, w_in_hbm, w_out_hbm,
+    lens_hbm, pair_hbm, w_in_hbm, w_out_hbm,
     updated, magnitude,
-    pair, w_in, w_out,
-    s_l, s_r, d_l, d_r, turned, s_t, d_t, normed, gates, w_proj, w_gate, w_last,
+    lens, pair, w_in, w_out,
+    s_l, s_r, d_l, d_r, turned, across, s_t, d_t, normed, gates, w_proj, w_gate, w_last,
     s_all, d_all,
     send_l, send_r, send_t, send_m, recv_l, recv_r, recv_t, recv_all,
     fetched, slab,
@@ -75,6 +75,7 @@
             pair_hbm.at[:, :, columns(2)], pair.at[:, :, columns(2)], fetched.at[2]
         ),
     ]
+    fetch.append(pltpu.make_async_copy(lens_hbm, lens, fetched.at[5]))
     for copy in fetch:
         copy.start()
 
@@ -91,6 +92,7 @@
             w_proj[rows, 0:128] = jnp.where(even, part, 0.0).astype(BF16)
             w_proj[rows, 128:256] = jnp.where(even, 0.0, part).astype(BF16)
 
+    fetch[5].wait()
     my_len = [lens[core * 4 + b] for b in range(4)]
     lane = lax.broadcasted_iota(jnp.int32, (8, 128), 1)
     sub = lax.broadcasted_iota(jnp.int32, (8, 128), 0)
@@ -100,11 +102,8 @@
         my_len[0],
         jnp.where(group == 1, my_len[1], jnp.where(group == 2, my_len[2], my_len[3])),
     )
-    s_l2 = s_l.reshape(36, 256, 128)
-    s_r2 = s_r.reshape(36, 256, 128)
     d_l2 = d_l.reshape(24, 384, 128)
     d_r2 = d_r.reshape(24, 384, 128)
-    d_t2 = d_t.reshape(36, 256, 128)
 
     def pair_rows(row, third):
         return jnp.concatenate(
@@ -135,7 +134,9 @@
             half_mask = jnp.where((i_lane < len_lane) & (k_sub < len_lane), 0.5, 0.0)
             value = out[0:256].reshape(32, 8, 128) * half_mask[None]
             gate = jnp.tanh(out[256:512]).reshape(32, 8, 128) + 1.0
-            store[third * 12 + q] = (value * gate).reshape(256, 128).astype(BF16)
+            store[third * 12 + q] = (
+                (value * gate).reshape(256, 128).astype(BF16).reshape(128, 2, 128)
+            )
             return carry
 
         steps(count, U_PROJ, body, 0)
@@ -157,7 +158,9 @@
             channel = (oz * 16 + oy * 4 + ox) * 2
             for c in range(2):
                 pltpu.make_async_remote_copy(
-                    src_ref=source.at[third, pl.ds(first, count), channel + c],
+                    src_ref=source.at[
+                        third * 12 + first : third * 12 + first + count, channel + c
+                    ],
                     dst_ref=target.at[c, third, x, pl.ds(gx * 12 + first, count)],
                     send_sem=send_sem,
                     recv_sem=recv_sem.at[third],
@@ -168,11 +171,11 @@
         to_others(send)
         for c in range(2):
             target[c, third, x, pl.ds(gx * 12 + first, count)] = source[
-                third, first : first + count, me * 2 + c
+                third * 12 + first : third * 12 + first + count, me * 2 + c
             ]
 
     def wait_part(sem, rows=12):
-        part = d_t.at[0, pl.ds(0, rows), pl.ds(0, 126)]
+        part = s_t.at[0, pl.ds(0, 63), :, pl.ds(0, rows)]
         pltpu.make_async_copy(part, part, sem).wait()
 
     for third in range(3):
@@ -181,7 +184,7 @@
             normalize(third, first, count)
             if third == 0 and first == 0:
                 prepare()
-            project(third, first, count, 0, s_l2)
+            project(third, first, count, 0, s_l)
             if third == 0 and first == 0:
                 pl.semaphore_wait(barrier, 64)
                 pl.semaphore_signal(
@@ -189,7 +192,7 @@
                 )
             send_part(third, first, count, s_l, d_l, send_l, recv_l)
     for third in range(3):
-        project(third, 0, 12, 512, s_r2)
+        project(third, 0, 12, 512, s_r)
         send_part(third, 0, 12, s_r, d_r, send_r, recv_r)
 
     fetch[2].wait()
@@ -236,14 +239,15 @@
     lane4 = lax.broadcasted_iota(jnp.int32, (32, 512), 1) % 128 // 32
 
     def multiply(third, after):
+        for c in range(2):
+            for col in range(4):
+                across[c, :, col * 128 : (col + 1) * 128] = d_r2[c * 12 + third * 4 + col]
+
         def body(r, carry):
             shift = lax.rem(r + 2 * core, 4)
             block = lax.rem(z + shift, 4)
             for c in range(2):
-                right = jnp.concatenate(
-                    [d_r2[c * 12 + third * 4 + col] for col in range(4)], axis=1
-                )
-                out = dot(turned[c * 4 + block], right, 1, 0)
+                out = dot(turned[c * 4 + block], across[c], 1, 0)
                 rows = []
                 for t in range(3):
                     g = [out[t * 128 + b * 32 : t * 128 + (b + 1) * 32] for b in range(4)]
@@ -257,7 +261,7 @@
                 full = jnp.concatenate(rows, axis=0)
                 for piece in range(4):
                     for col in range(4):
-                        s_t[third, block * 4 + piece, col, :, c] = (
+                        s_t[third, (block * 4 + piece) * 4 + col, c] = (
                             full[piece * 24 : (piece + 1) * 24, col * 128 : (col + 1) * 128]
                             .astype(BF16)
                             .reshape(12, 2, 128)
@@ -267,17 +271,32 @@
             return carry
 
         lax.fori_loop(1, 5, body, 0)
-        d_t[third, :, pl.ds(me * 2, 2)] = s_t[third, gx, x]
+        whole = d_t.at[
+            third * 12 : third * 12 + 12, pl.ds(pl.multiple_of(me // 2 * 8, 8), 8)
+        ]
+        for half in range(2):
+
+            @pl.when(me % 2 == half)
+            def _():
+                for c in range(2):
+                    whole[:, half * 4 + 2 * c : half * 4 + 2 * c + 2] = s_t[
+                        third, gx * 4 + x, c
+                    ]
+
 
     def send_back(third, oz, oy, ox, first, count, sem):
-        pltpu.make_async_remote_copy(
-            src_ref=s_t.at[third, oz * 4 + oy, ox, pl.ds(first, count)],
-            dst_ref=d_t.at[third, pl.ds(first, count), pl.ds(me * 2, 2)],
-            send_sem=send_t,
-            recv_sem=sem,
-            device_id=(core, oz, oy, ox),
-            device_id_type=MESH_ID,
-        ).start()
+        for c in range(2):
+            pltpu.make_async_remote_copy(
+                src_ref=s_t.at[third, (oz * 4 + oy) * 4 + ox, c, first : first + count],
+                dst_ref=d_t.at[
+                    third * 12 + first : third * 12 + first + count,
+                    pl.ds(pl.multiple_of(me * 4 + 2 * c, 2), 2),
+                ],
+                send_sem=send_t,
+                recv_sem=sem,
+                device_id=(core, oz, oy, ox),
+                device_id_type=MESH_ID,
+            ).start()
 
     def send_block(third, block, own, first, count, sem):
         def body(n, carry):
@@ -298,17 +317,20 @@
 
     def finish(third, first, count, total):
         def body(q, total):
-            v = d_t2[third * 12 + q].astype(F32).reshape(32, 8, 128)
+            v = d_t[third * 12 + q].astype(F32)
 
             def over_channels(array):
-                s = jnp.sum(array, axis=0)
+                parts = [array[n * 8 : n * 8 + 8] for n in range(32)]
+                while len(parts) > 1:
+                    parts = [parts[n] + parts[n + 1] for n in range(0, len(parts), 2)]
+                s = parts[0]
                 s = s + pltpu.roll(s, 4, 0)
                 s = s + pltpu.roll(s, 2, 0)
-                return s * (1.0 / 128)
-
-            v = v - over_channels(v)[None]
-            v = v * lax.rsqrt(over_channels(v * v) + EPS)[None]
-            out = dot(v.reshape(256, 128).astype(BF16), w_last[...], 0, 0)
+                return jnp.concatenate([s * (1.0 / 128)] * 32, axis=0)
+
+            v = v - over_channels(v)
+            v = v * lax.rsqrt(over_channels(v * v) + EPS)
+            out = dot(v.astype(BF16), w_last[...], 0, 0)
             change = out * gates[third * 12 + q]
             for parity in range(2):
                 new = pair_rows(2 * q + parity, third).astype(F32)
@@ -376,21 +398,23 @@
         lambda *refs: kernel(entries, *refs),
         out_shape=(
             pltpu.VMEM(pair_repr.shape, BF16),
-            jax.ShapeDtypeStruct((1, 1), F32),
+            pltpu.VMEM((1, 1), F32),
         ),
-        in_specs=[pl.BlockSpec(memory_space=pltpu.SMEM), hbm, hbm, hbm],
+        in_specs=[hbm, hbm, hbm, hbm],
         out_specs=(vmem, vmem),
         scratch_shapes=[
+            pltpu.SMEM(seq_lengths.shape, jnp.int32),
             pltpu.VMEM(pair_repr.shape, BF16),
             pltpu.VMEM(weight_in.shape, BF16),
             pltpu.VMEM(weight_out.shape, BF16),
-            pltpu.VMEM((3, 12, 128, 2, 128), BF16),
-            pltpu.VMEM((3, 12, 128, 2, 128), BF16),
+            pltpu.VMEM((36, 128, 2, 128), BF16),
+            pltpu.VMEM((36, 128, 2, 128), BF16),
             pltpu.VMEM((2, 3, 4, 192, 2, 128), BF16),
             pltpu.VMEM((2, 3, 4, 192, 2, 128), BF16),
             pltpu.VMEM((8, 384, 384), BF16),
-            pltpu.VMEM((3, 16, 4, 12, 2, 2, 128), BF16),
-            pltpu.VMEM((3, 12, 128, 2, 128), BF16),
+            pltpu.VMEM((2, 384, 512), BF16),
+            pltpu.VMEM((3, 64, 2, 12, 2, 128), BF16),
+            pltpu.VMEM((36, 256, 128), BF16),
             pltpu.VMEM((36, 128, 256), BF16),
             pltpu.VMEM((36, 128, 256), F32),
             pltpu.VMEM((1024, 256), BF16),
@@ -406,7 +430,7 @@
             dma((3,)),
             dma((5,)),
             dma,
-            dma((5,)),
+            dma((6,)),
             pltpu.SemaphoreType.REGULAR,
         ],
         compiler_params=pltpu.CompilerParams(

time: 105 us -> 101 us (0.962)
  Pallas kernels: 101 us -> 97.2 us
    pallas_call x1, Pallas kernels: 101 us -> 97.2 us  [per_device(): pl.pallas_call(lambda *refs: kernel(entries, *refs), out_shape=(pltpu.VME...]
where the time goes in v4:
time: 101 us; the launch traced here: 100 us
  Pallas kernels  97.2 us (96%)
  between operations  1.8 us (2%)
  local copies, waits for them, and re-layouts  1.41 us (1%)
    pallas_call x1, Pallas kernels, per_device(): pl.pallas_call(lambda *refs: kernel(entries, *refs), out_shape=(pltpu.VME...  97.2 us

profile of v4, /device:TPU:1, one launch (start us, length us, event | category | flops | bytes accessed | tf_op | source)
XLA Modules:
  0.0 100.4 jit_solution(8839678461561282717)
XLA Ops:
  0.6 97.2 %triangle.1 = (bf16[4,24,96,128]{3,2,1,0:T(8,128)(2,1)S(1)}, f32[1,1]{1,0:T(1,128)S(1)}) custom-call(s32[8]{0:T(128)} %refs_0_.1, bf16[4,24,96,128]{3,2,1,0:T(8,128)(2,1)} %refs_1_.1, bf16[128,640]{1,0:T(8,128)(2,1)} %refs_2_.1, bf16[128,128]{1,0:T(8,128)(2,1)} %refs_3_.1), custom_call_target="tpu_custom_call" | custom-call | tf_op jit(solution)/shard_map/triangle/pallas_call | solution.py:397
  97.8 1.4 %copy.8 = bf16[4,24,96,128]{3,2,1,0:T(8,128)(2,1)} copy(bf16[4,24,96,128]{3,2,1,0:T(8,128)(2,1)S(1)} %get-tuple-element.6) | data formatting | bytes 4718592

commit v5 on v4

--- a/solution.py
+++ b/solution.py
@@ -32,9 +32,8 @@
 
 
 def kernel(
-    entries,
     lens_hbm, pair_hbm, w_in_hbm, w_out_hbm,
-    updated, magnitude,
+    updated, sums,
     lens, pair, w_in, w_out,
     s_l, s_r, d_l, d_r, turned, across, s_t, d_t, normed, gates, w_proj, w_gate, w_last,
     s_all, d_all,
@@ -44,6 +43,26 @@
     core, z, y, x = (lax.axis_index(a) for a in AXES)
     gx = z * 4 + y
     me = gx * 4 + x
+
+    def columns(third):
+        return pl.ds(third * 32, 32)
+
+    fetch = [
+        pltpu.make_async_copy(
+            pair_hbm.at[:, :, columns(0)], pair.at[:, :, columns(0)], fetched.at[0]
+        ),
+        pltpu.make_async_copy(w_in_hbm, w_in, fetched.at[3]),
+        pltpu.make_async_copy(w_out_hbm, w_out, fetched.at[4]),
+        pltpu.make_async_copy(
+            pair_hbm.at[:, :, columns(1)], pair.at[:, :, columns(1)], fetched.at[1]
+        ),
+        pltpu.make_async_copy(
+            pair_hbm.at[:, :, columns(2)], pair.at[:, :, columns(2)], fetched.at[2]
+        ),
+    ]
+    fetch.append(pltpu.make_async_copy(lens_hbm, lens, fetched.at[5]))
+    for copy in fetch:
+        copy.start()
 
     barrier = pltpu.get_barrier_semaphore()
     zs = [lax.rem(z + n, 4) for n in range(4)]
@@ -59,25 +78,6 @@
         if step[0] == 0 or step == (1, 0, 0, 0):
             pl.semaphore_signal(barrier, inc=1, device_id=device, device_id_type=MESH_ID)
 
-    def columns(third):
-        return pl.ds(third * 32, 32)
-
-    fetch = [
-        pltpu.make_async_copy(
-            pair_hbm.at[:, :, columns(0)], pair.at[:, :, columns(0)], fetched.at[0]
-        ),
-        pltpu.make_async_copy(w_in_hbm, w_in, fetched.at[3]),
-        pltpu.make_async_copy(w_out_hbm, w_out, fetched.at[4]),
-        pltpu.make_async_copy(
-            pair_hbm.at[:, :, columns(1)], pair.at[:, :, columns(1)], fetched.at[1]
-        ),
-        pltpu.make_async_copy(
-            pair_hbm.at[:, :, columns(2)], pair.at[:, :, columns(2)], fetched.at[2]
-        ),
-    ]
-    fetch.append(pltpu.make_async_copy(lens_hbm, lens, fetched.at[5]))
-    for copy in fetch:
-        copy.start()
 
     row2 = lax.broadcasted_iota(jnp.int32, (256, 128), 0)
     col2 = lax.broadcasted_iota(jnp.int32, (256, 128), 1)
@@ -142,11 +142,14 @@
         steps(count, U_PROJ, body, 0)
 
     def to_others(send):
+        sign = 1 + 2 * core
+        mirrored = [lax.rem(x + dx * sign, 4) for dx in range(4)]
+
         def body(n, carry):
-            oz = lax.rem(z + n, 4)
-            oy = lax.rem(y + n // 4, 4)
+            oz = z + n * sign
+            oy = y + n // 4 * sign
             for dx in range(4):
-                send(lax.rem(oz + dx, 4), lax.rem(oy + dx, 4), xs[dx])
+                send(lax.rem(oz + dx * sign, 4), lax.rem(oy + dx * sign, 4), mirrored[dx])
             return carry
 
         lax.fori_loop(1, 16, body, 0)
@@ -168,14 +171,15 @@
                     device_id_type=MESH_ID,
                 ).start()
 
-        to_others(send)
         for c in range(2):
             target[c, third, x, pl.ds(gx * 12 + first, count)] = source[
                 third * 12 + first : third * 12 + first + count, me * 2 + c
             ]
 
+        to_others(send)
+
     def wait_part(sem, rows=12):
-        part = s_t.at[0, pl.ds(0, 63), :, pl.ds(0, rows)]
+        part = s_t.at[0, pl.ds(0, 63), pl.ds(0, rows)]
         pltpu.make_async_copy(part, part, sem).wait()
 
     for third in range(3):
@@ -239,13 +243,20 @@
     lane4 = lax.broadcasted_iota(jnp.int32, (32, 512), 1) % 128 // 32
 
     def multiply(third, after):
+        def place(r):
+            shift = lax.rem(r + 2 * core, 4)
+            return lax.rem(z + shift, 4), jnp.where(shift == 0, 1, 0)
+
+        def leave(r):
+            after(*place(r))
+
         for c in range(2):
             for col in range(4):
                 across[c, :, col * 128 : (col + 1) * 128] = d_r2[c * 12 + third * 4 + col]
 
         def body(r, carry):
-            shift = lax.rem(r + 2 * core, 4)
-            block = lax.rem(z + shift, 4)
+            block = place(r)[0]
+            full = []
             for c in range(2):
                 out = dot(turned[c * 4 + block], across[c], 1, 0)
                 rows = []
@@ -258,16 +269,17 @@
                             jnp.where(lane4 == 1, g[1], jnp.where(lane4 == 2, g[2], g[3])),
                         )
                     )
-                full = jnp.concatenate(rows, axis=0)
-                for piece in range(4):
-                    for col in range(4):
-                        s_t[third, (block * 4 + piece) * 4 + col, c] = (
-                            full[piece * 24 : (piece + 1) * 24, col * 128 : (col + 1) * 128]
-                            .astype(BF16)
-                            .reshape(12, 2, 128)
-                        )
-
-            after(block, jnp.where(shift == 0, 1, 0))
+                full.append(jnp.concatenate(rows, axis=0))
+            for piece in range(4):
+                for col in range(4):
+                    here = [
+                        f[piece * 24 : (piece + 1) * 24, col * 128 : (col + 1) * 128]
+                        .astype(BF16)
+                        .reshape(12, 2, 128)
+                        for f in full
+                    ]
+                    s_t[third, (block * 4 + piece) * 4 + col] = jnp.concatenate(here, axis=1)
+            leave(r)
             return carry
 
         lax.fori_loop(1, 5, body, 0)
@@ -278,25 +290,21 @@
 
             @pl.when(me % 2 == half)
             def _():
-                for c in range(2):
-                    whole[:, half * 4 + 2 * c : half * 4 + 2 * c + 2] = s_t[
-                        third, gx * 4 + x, c
-                    ]
+                whole[:, half * 4 : half * 4 + 4] = s_t[third, gx * 4 + x]
 
 
     def send_back(third, oz, oy, ox, first, count, sem):
-        for c in range(2):
-            pltpu.make_async_remote_copy(
-                src_ref=s_t.at[third, (oz * 4 + oy) * 4 + ox, c, first : first + count],
-                dst_ref=d_t.at[
-                    third * 12 + first : third * 12 + first + count,
-                    pl.ds(pl.multiple_of(me * 4 + 2 * c, 2), 2),
-                ],
-                send_sem=send_t,
-                recv_sem=sem,
-                device_id=(core, oz, oy, ox),
-                device_id_type=MESH_ID,
-            ).start()
+        pltpu.make_async_remote_copy(
+            src_ref=s_t.at[third, (oz * 4 + oy) * 4 + ox, first : first + count],
+            dst_ref=d_t.at[
+                third * 12 + first : third * 12 + first + count,
+                pl.ds(pl.multiple_of(me * 4, 4), 4),
+            ],
+            send_sem=send_t,
+            recv_sem=sem,
+            device_id=(core, oz, oy, ox),
+            device_id_type=MESH_ID,
+        ).start()
 
     def send_block(third, block, own, first, count, sem):
         def body(n, carry):
@@ -350,8 +358,8 @@
     wait_part(recv_r.at[0])
     multiply(0, hold)
     wait_part(recv_r.at[1])
+    send_third(0, 0, 12, recv_t.at[0])
     multiply(1, hold)
-    send_third(0, 0, 12, recv_t.at[0])
     wait_part(recv_r.at[2])
     send_third(1, 0, 12, recv_t.at[1])
     multiply(2, lambda block, own: send_block(2, block, own, 0, 6, recv_t.at[2]))
@@ -385,20 +393,29 @@
         ).start()
     rest = d_all.at[pl.ds(0, 127)]
     pltpu.make_async_copy(rest, rest, recv_all).wait()
-    everyone = jnp.sum(d_all.reshape(128, 128)[...], axis=0, keepdims=True)
-    magnitude[...] = jnp.sum(everyone, axis=1, keepdims=True) * (1.0 / entries)
+    sums[...] = jnp.sum(d_all.reshape(128, 128)[...].reshape(16, 8, 128), axis=0)
     pltpu.make_async_copy(rest, rest, send_m).wait()
+
+
+def hand_over(entries, updated, sums, out, total, done):
+    copies = [pltpu.make_async_copy(updated.at[b], out.at[b], done.at[b]) for b in range(4)]
+    for copy in copies:
+        copy.start()
+    everyone = jnp.sum(sums[...], axis=0, keepdims=True)
+    total[...] = jnp.sum(everyone, axis=1, keepdims=True) * (1.0 / entries)
+    for copy in copies:
+        copy.wait()
 
 
 def per_device(entries, pair_repr, seq_lengths, weight_in, weight_out):
     vmem = pl.BlockSpec(memory_space=pltpu.VMEM)
     hbm = pl.BlockSpec(memory_space=pl.ANY)
     dma = pltpu.SemaphoreType.DMA
-    updated, magnitude = pl.pallas_call(
-        lambda *refs: kernel(entries, *refs),
+    updated, sums = pl.pallas_call(
+        kernel,
         out_shape=(
             pltpu.VMEM(pair_repr.shape, BF16),
-            pltpu.VMEM((1, 1), F32),
+            pltpu.VMEM((8, 128), F32),
         ),
         in_specs=[hbm, hbm, hbm, hbm],
         out_specs=(vmem, vmem),
@@ -413,7 +430,7 @@
             pltpu.VMEM((2, 3, 4, 192, 2, 128), BF16),
             pltpu.VMEM((8, 384, 384), BF16),
             pltpu.VMEM((2, 384, 512), BF16),
-            pltpu.VMEM((3, 64, 2, 12, 2, 128), BF16),
+            pltpu.VMEM((3, 64, 12, 4, 128), BF16),
             pltpu.VMEM((36, 256, 128), BF16),
             pltpu.VMEM((36, 128, 256), BF16),
             pltpu.VMEM((36, 128, 256), F32),
@@ -438,7 +455,19 @@
         ),
         name="triangle",
     )(seq_lengths, pair_repr, weight_in, weight_out)
-    return updated, magnitude.reshape(())
+    out, total = pl.pallas_call(
+        lambda *refs: hand_over(entries, *refs),
+        out_shape=(
+            jax.ShapeDtypeStruct(pair_repr.shape, BF16),
+            jax.ShapeDtypeStruct((1, 1), F32),
+        ),
+        in_specs=[vmem, vmem],
+        out_specs=(hbm, vmem),
+        scratch_shapes=[dma((4,))],
+        compiler_params=pltpu.CompilerParams(vmem_limit_bytes=2**20),
+        name="hand_over",
+    )(updated, sums)
+    return out, total.reshape(())
 
 
 def solution(mesh):

time: 101 us -> 99.6 us (0.986)
  Pallas kernels: 97.2 us -> 98.8 us
  local copies, waits for them, and re-layouts: 1.41 us -> 0 us
  between operations: 1.8 us -> 0.64 us
    pallas_call x1 -> x2, Pallas kernels: 97.2 us -> 98.8 us  [the longest x1 96.9 us: per_device(): pl.pallas_call(kernel, out_shape=(pltpu.VMEM(pair_repr.shape, BF16), pltp...]
    unnamed x1 -> x0, local copies, waits for them, and re-layouts: 1.41 us -> none
where the time goes in v5:
time: 99.6 us; the launch traced here: 99.5 us
  Pallas kernels  98.8 us (99%)
    pallas_call x1, Pallas kernels, per_device(): pl.pallas_call(kernel, out_shape=(pltpu.VMEM(pair_repr.shape, BF16), pltp...  96.9 us

profile of v5, /device:TPU:1, one launch (start us, length us, event | category | flops | bytes accessed | tf_op | source)
XLA Modules:
  0.0 99.5 jit_solution(9588179676801060595)
XLA Ops:
  0.6 96.9 %triangle.1 = (bf16[4,24,96,128]{3,2,1,0:T(8,128)(2,1)S(1)}, f32[8,128]{1,0:T(8,128)S(1)}) custom-call(s32[8]{0:T(128)} %lens_hbm.1, bf16[4,24,96,128]{3,2,1,0:T(8,128)(2,1)} %pair_hbm.1, bf16[128,640]{1,0:T(8,128)(2,1)} %w_in_hbm.1, bf16[128,128]{1,0:T(8,128)(2,1)} %w_out_hbm.1), custom_call_target="tpu_custom_call" | custom-call | tf_op jit(solution)/shard_map/triangle/pallas_call | solution.py:414
  97.5 1.9 %hand_over.1 = (bf16[4,24,96,128]{3,2,1,0:T(8,128)(2,1)}, f32[1,1]{1,0:T(1,128)}) custom-call(bf16[4,24,96,128]{3,2,1,0:T(8,128)(2,1)S(1)} %get-tuple-element.6.refs_0_, f32[8,128]{1,0:T(8,128)S(1)} %get-tuple-element.7.refs_1_), custom_call_target="tpu_custom_call" | custom-call | tf_op jit(solution)/shard_map/hand_over/pallas_call | solution.py:458

commit v6 on v5

--- a/solution.py
+++ b/solution.py
@@ -350,7 +350,7 @@
                 total = total + jnp.sum(jnp.abs(new.astype(F32)).reshape(16, 8, 128), axis=0)
             return total
 
-        return steps(count, 3 if count == 3 else U_LAST, lambda n, carry: body(first + n, carry), total)
+        return steps(count, 3 if count in (3, 9) else U_LAST, lambda n, carry: body(first + n, carry), total)
 
     def hold(block, own):
         pass
@@ -362,16 +362,16 @@
     multiply(1, hold)
     wait_part(recv_r.at[2])
     send_third(1, 0, 12, recv_t.at[1])
-    multiply(2, lambda block, own: send_block(2, block, own, 0, 6, recv_t.at[2]))
-    send_third(2, 6, 6, recv_t.at[3])
+    multiply(2, lambda block, own: send_block(2, block, own, 0, 9, recv_t.at[2]))
+    send_third(2, 9, 3, recv_t.at[3])
     total = jnp.zeros((8, 128), F32)
     for third in range(2):
         wait_part(recv_t.at[third])
         total = finish(third, 0, 12, total)
-    wait_part(recv_t.at[2], 6)
-    total = finish(2, 0, 6, total)
-    wait_part(recv_t.at[3], 6)
-    total = finish(2, 6, 6, total)
+    wait_part(recv_t.at[2], 9)
+    total = finish(2, 0, 9, total)
+    wait_part(recv_t.at[3], 3)
+    total = finish(2, 9, 3, total)
 
     flat = core * 64 + me
     mine = jnp.sum(total, axis=0, keepdims=True)

time: 99.6 us -> 99.5 us (level)
  no operation moved by 1% of the time
where the time goes in v6:
time: 99.5 us; the launch traced here: 99.4 us
  Pallas kernels  98.7 us (99%)
    pallas_call x1, Pallas kernels, per_device(): pl.pallas_call(kernel, out_shape=(pltpu.VMEM(pair_repr.shape, BF16), pltp...  96.8 us

profile of v6, /device:TPU:1, one launch (start us, length us, event | category | flops | bytes accessed | tf_op | source)
XLA Modules:
  0.0 99.4 jit_solution(12138708949826437402)
XLA Ops:
  0.6 96.8 %triangle.1 = (bf16[4,24,96,128]{3,2,1,0:T(8,128)(2,1)S(1)}, f32[8,128]{1,0:T(8,128)S(1)}) custom-call(s32[8]{0:T(128)} %lens_hbm.1, bf16[4,24,96,128]{3,2,1,0:T(8,128)(2,1)} %pair_hbm.1, bf16[128,640]{1,0:T(8,128)(2,1)} %w_in_hbm.1, bf16[128,128]{1,0:T(8,128)(2,1)} %w_out_hbm.1), custom_call_target="tpu_custom_call" | custom-call | tf_op jit(solution)/shard_map/triangle/pallas_call | solution.py:414
  97.4 1.9 %hand_over.1 = (bf16[4,24,96,128]{3,2,1,0:T(8,128)(2,1)}, f32[1,1]{1,0:T(1,128)}) custom-call(bf16[4,24,96,128]{3,2,1,0:T(8,128)(2,1)S(1)} %get-tuple-element.6.refs_0_, f32[8,128]{1,0:T(8,128)S(1)} %get-tuple-element.7.refs_1_), custom_call_target="tpu_custom_call" | custom-call | tf_op jit(solution)/shard_map/hand_over/pallas_call | solution.py:458
